TPU v7x, 512 devices: a whole 4x8x8 slice. The times are simulated.
512 devices in a mesh: row: 16 (over x_hi, y), col: 32 (over x_lo, z, core).
Axes of the slice: x: 4 (x_hi: 2, x_lo: 2; x = x_hi * 2 + x_lo), y: 8, z: 8, core: 2. Of those that a mesh axis runs over, the one named last changes fastest.
Arguments:
- fact_block: int32 [1572864, 1], P(('row', 'col')), may hold values from 0 to 511; in each aligned block of 3072 rows (0 to 3071, 3072 to 6143, ...) at most 12 rows name the same one
- fact_offset: int32 [1572864], P(('row', 'col')), may hold values from 0 to 2047
- fact_date: int32 [1572864], P(('row', 'col')), may hold values from 0 to 2555
- revenue: bfloat16 [1572864], P(('row', 'col')), may hold values from 0.5 to 4
- supplier_words: int32 [35328], P('col'), may hold values from 0 to 1073741823
- date_words: int32 [96], P('col'), may hold values from 0 to 1073741823
- candidates: int32 [1024], replicated, may hold values from 0 to 1048575
Outputs:
- supplier_revenue: float32 [1048576], P(('row', 'col'))
- candidate_revenue: float32 [1024], replicated
- candidate_total: float32 [], replicated
Inputs may be any that keep to these rules, and one draw needn't show every extreme that they name: `fact_block`: each device's rows name no owner block more than 12 times. `candidates`: ids may repeat.
All inputs are finite; a program needn't handle non-finite values.
Results may differ from a plain program's by a relative error of at most 0.0003.
Values sent between devices are 32-bit elements; how exact they have to be, the bound alone decides.
No kernel may reach another device: no remote copies, remote signals or barrier semaphores. Data moves between devices by JAX's collectives and lax.ppermute only.
A program may use at most 64 MiB of HBM per device.

v0:
```python
import jax
import jax.numpy as jnp
from jax import lax
from jax.sharding import Mesh
from jax.sharding import PartitionSpec as P

SUP_DEV = 2048
ROW = ("row_0", "row_1")
COL = ("col_0", "col_1", "col_2")
ROW_COL = ("row_0", "row_1", "col_0", "col_1", "col_2")


def copy_for_each(x, axis):
    copies = jnp.broadcast_to(x, (lax.axis_size(axis), *x.shape))
    return lax.all_to_all(copies, axis, split_axis=0, concat_axis=0, tiled=True)


def joined_along(parts, dim):
    lengths = list(parts.shape[1:])
    lengths[dim] *= parts.shape[0]
    return jnp.moveaxis(parts, 0, dim).reshape(lengths)


def gather_directly(x, axis, dim):
    parts = copy_for_each(x, axis)
    return joined_along(parts, dim)


def over_axes(x, axes):
    for axis in axes:
        x = lax.psum(x, axis)
    return x


def filtered_revenue(owner, fact_offset, fact_date, revenue, supplier_all, date_all):
    words_per_block = (SUP_DEV + 29) // 30
    word_index = owner * words_per_block + fact_offset // 30
    supplier_word = jnp.take(supplier_all, word_index)
    supplier_bit = jnp.bitwise_and(jnp.right_shift(supplier_word, fact_offset % 30), 1)
    date_slot = fact_date // 30
    positions = jnp.arange(date_all.shape[0], dtype=jnp.int32)
    date_word = jnp.sum(
        jnp.where(date_slot[:, None] == positions[None, :], date_all[None, :], 0), axis=1
    )
    date_bit = jnp.bitwise_and(jnp.right_shift(date_word, fact_date % 30), 1)
    return jnp.where(supplier_bit * date_bit == 1, revenue, jnp.zeros_like(revenue))


def per_device(fact_block, fact_offset, fact_date, revenue, supplier_words, date_words, candidates):
    devices = lax.axis_size(ROW) * lax.axis_size(COL)
    supplier_all, date_all = (
        gather_directly(supplier_words, COL, 0),
        gather_directly(date_words, COL, 0),
    )
    owner = fact_block[:, 0]
    masked = filtered_revenue(owner, fact_offset, fact_date, revenue, supplier_all, date_all)
    row_count = fact_offset.shape[0]
    capacity = max(2, 2 * row_count // devices)
    row_ids = jnp.arange(row_count, dtype=jnp.int32)
    earlier = (owner[:, None] == owner[None, :]) & (row_ids[None, :] < row_ids[:, None])
    ranking = jnp.sum(earlier, axis=1, dtype=jnp.int32)
    slot_index = owner * capacity + ranking
    slot_revenue = (
        jnp.zeros((devices * capacity,), jnp.float32).at[slot_index].set(masked.astype(jnp.float32))
    )
    slot_offset = (
        jnp.zeros((devices * capacity,), jnp.float32)
        .at[slot_index]
        .set(fact_offset.astype(jnp.float32))
    )
    payload = jnp.stack((slot_revenue, slot_offset), axis=-1)
    payload = payload.reshape(lax.axis_size(ROW), lax.axis_size(COL), 2 * capacity)
    arrived = lax.all_to_all(
        lax.all_to_all(payload, COL, split_axis=1, concat_axis=1, tiled=True),
        ROW,
        split_axis=0,
        concat_axis=0,
        tiled=True,
    )
    arrived = arrived.reshape(-1, 2)
    owned = jax.ops.segment_sum(
        arrived[:, 0], arrived[:, 1].astype(jnp.int32), num_segments=SUP_DEV
    )
    global_id = owner * SUP_DEV + fact_offset
    onehot_cands = (global_id[:, None] == candidates[None, :]).astype(jnp.bfloat16)
    own_terms = jnp.dot(masked[None, :], onehot_cands, preferred_element_type=jnp.float32)[0]
    candidate_revenue = over_axes(own_terms, ROW_COL)
    candidate_total = jnp.sum(candidate_revenue)
    return (owned, candidate_revenue, candidate_total)


def solution(mesh):
    split = Mesh(mesh.devices.reshape(2, 8, 2, 8, 2), ("row_0", "row_1", "col_0", "col_1", "col_2"))
    return jax.shard_map(
        per_device,
        mesh=split,
        in_specs=(P(ROW_COL, None), P(ROW_COL), P(ROW_COL), P(ROW_COL), P(COL), P(COL), P()),
        out_specs=(P(ROW_COL), P(), P()),
        check_vma=False,
    )
```

profile of v0, /device:TPU:1, one launch (start us, length us, event | category | flops | bytes accessed | tf_op | source)
XLA Modules:
  0.0 199.4 jit_solution(4576482019518081585)
XLA Ops:
  0.6 1.3 broadcast_in_dim.48
  1.9 12.9 %all-to-all-start.1 = ((s32[32,1,3]{2,1,0:T(1,128)}), s32[32,1,3]{2,1,0:T(1,128)S(1)}, u32[]{:S(2)}, u32[]{:S(2)}) async-start(s32[32,1,3]{2,1,0:T(1,128)} %broadcast_in_dim.48), calls=%async_computation.1 | async-start | bytes 32768 | tf_op jit(solution)/shard_map/all_to_all | solution.py:15
  14.8 3.9 %convert_reduce_fusion = s32[3072]{0:T(1024)S(1)} fusion(s32[3072]{0:T(1024)} %bitcast.19), kind=kLoop, calls=%fused_computation.4 | loop fusion | flops 47182848 | bytes 24576 | tf_op jit(solution)/shard_map/reduce_sum | solution.py:61
  18.6 0.7 compare_select_fusion
  19.4 0.8 multiply_add_fusion
  20.2 11.8 %scatter_custom_fusion.1 = f32[6144]{0:T(1024)S(1)} fusion(s32[3072]{0:T(1024)S(1)} %bitcast.24, f32[3072]{0:T(1024)S(1)} %get-tuple-element.7, f32[]{:T(128)} %constant.30.clone.1), kind=kCustom, calls=%fused_computation.33 | custom fusion | bytes 24580 | tf_op jit(solution)/shard_map/scatter | solution.py:69
  32.0 1.4 broadcast_in_dim.45
  33.4 8.3 %all-to-all-start = ((s32[32,1,1104]{2,1,0:T(1,128)}), s32[32,1,1104]{2,1,0:T(1,128)S(1)}, u32[]{:S(2)}, u32[]{:S(2)}) async-start(s32[32,1,1104]{2,1,0:T(1,128)} %broadcast_in_dim.45), calls=%async_computation | async-start | bytes 294912 | tf_op jit(solution)/shard_map/all_to_all | solution.py:15
  41.8 0.7 add_select_fusion.1
  43.0 0.7 reduce.8
  44.1 7.0 %all-to-all-done = s32[32,1,1104]{2,1,0:T(1,128)S(1)} async-done(((s32[32,1,1104]{2,1,0:T(1,128)}), s32[32,1,1104]{2,1,0:T(1,128)S(1)}, u32[]{:S(2)}, u32[]{:S(2)}) %all-to-all-start) | async-done | bytes 141344 | tf_op jit(solution)/shard_map/all_to_all | solution.py:15
  51.6 17.4 %gather_fusion = s32[3072]{0:T(1024)S(1)} fusion(s32[35328]{0:T(1024)S(1)} %reshape.40, s32[3072]{0:T(1024)S(1)} %get-tuple-element.6), kind=kCustom, calls=%fused_computation | custom fusion | bytes 36864 | tf_op jit(solution)/shard_map/jit(_take)/gather | solution.py:38
  69.1 11.8 %scatter_custom_fusion = f32[6144]{0:T(1024)S(1)} fusion(s32[3072]{0:T(1024)S(1)} %bitcast.25, f32[3072]{0:T(1024)S(1)} %get-tuple-element.3, f32[]{:T(128)} %constant.30.clone.1), kind=kCustom, calls=%fused_computation.35 | custom fusion | bytes 24580 | tf_op jit(solution)/shard_map/scatter | solution.py:64
  81.0 1.1 copy.15
  82.0 0.8 reshape.41
  83.0 0.8 reshape.96
  83.9 5.2 %all-to-all-start.2 = ((f32[32,1,384]{2,1,0:T(1,128)}), f32[32,1,384]{2,1,0:T(1,128)S(1)}, u32[]{:S(2)}, u32[]{:S(2)}) async-start(f32[32,1,384]{2,1,0:T(1,128)} %reshape.96), calls=%async_computation.2 | async-start | bytes 98304 | tf_op jit(solution)/shard_map/all_to_all | solution.py:74
  89.1 8.1 %all-to-all-done.2 = f32[32,1,384]{2,1,0:T(1,128)S(1)} async-done(((f32[32,1,384]{2,1,0:T(1,128)}), f32[32,1,384]{2,1,0:T(1,128)S(1)}, u32[]{:S(2)}, u32[]{:S(2)}) %all-to-all-start.2) | async-done | bytes 49184 | tf_op jit(solution)/shard_map/all_to_all | solution.py:74
  97.7 0.8 reduce.9
  98.8 0.8 reshape.98
  99.5 9.1 %all-to-all-start.3 = ((f32[16,1,768]{2,1,0:T(1,128)}), f32[16,1,768]{2,1,0:T(1,128)S(1)}, u32[]{:S(2)}, u32[]{:S(2)}) async-start(f32[16,1,768]{2,1,0:T(1,128)} %reshape.98), calls=%async_computation.3 | async-start | bytes 98304 | tf_op jit(solution)/shard_map/all_to_all | solution.py:73
  108.7 2.0 %fusion.1 = f32[1,1024]{1,0:T(1,128)S(1)} fusion(bf16[3072,1]{0,1:T(2,128)(2,1)S(1)} %reshape.76, s32[1024]{0:T(1024)S(1)} %copy-done.5, s32[3072]{0:T(1024)S(1)} %get-tuple-element.5), kind=kOutput, calls=%fused_computation.7 | convolution fusion | flops 9437184 | bytes 26624 | tf_op jit(solution)/shard_map/dot_general | solution.py:86
  110.7 5.6 %psum.35 = f32[1024]{0:T(1024)S(1)} all-reduce(f32[1024]{0:T(1024)S(1)} %bitcast.27), channel_id=1, replica_groups=mesh['row_0'=2,'row_1'=8,'col_0'=2,'col_1'=8,'col_2'=2] {'row_0'}, use_global_device_ids=true, to_apply=%region_5.6 | all-reduce | flops 1024 | bytes 8192 | tf_op jit(solution)/shard_map/psum | solution.py:31
  116.2 13.2 %psum.36 = f32[1024]{0:T(1024)S(1)} all-reduce(f32[1024]{0:T(1024)S(1)} %psum.35), channel_id=1, replica_groups=mesh['row_0'=2,'row_1'=8,'col_0'=2,'col_1'=8,'col_2'=2] {'row_1'}, use_global_device_ids=true, to_apply=%region_6.7 | all-reduce | flops 1024 | bytes 8192 | tf_op jit(solution)/shard_map/psum | solution.py:31
  129.4 3.8 %psum.37 = f32[1024]{0:T(1024)S(1)} all-reduce(f32[1024]{0:T(1024)S(1)} %psum.36), channel_id=1, replica_groups=mesh['row_0'=2,'row_1'=8,'col_0'=2,'col_1'=8,'col_2'=2] {'col_0'}, use_global_device_ids=true, to_apply=%region_7.8 | all-reduce | flops 1024 | bytes 8192 | tf_op jit(solution)/shard_map/psum | solution.py:31
  133.2 11.3 %psum.38 = f32[1024]{0:T(1024)S(1)} all-reduce(f32[1024]{0:T(1024)S(1)} %psum.37), channel_id=1, replica_groups=mesh['row_0'=2,'row_1'=8,'col_0'=2,'col_1'=8,'col_2'=2] {'col_1'}, use_global_device_ids=true, to_apply=%region_8.9 | all-reduce | flops 1024 | bytes 8192 | tf_op jit(solution)/shard_map/psum | solution.py:31
  144.5 12.9 %psum.39 = f32[1024]{0:T(1024)S(1)} all-reduce(f32[1024]{0:T(1024)S(1)} %psum.38), channel_id=1, replica_groups=mesh['row_0'=2,'row_1'=8,'col_0'=2,'col_1'=8,'col_2'=2] {'col_2'}, use_global_device_ids=true, to_apply=%region_9.10 | all-reduce | flops 1024 | bytes 8192 | tf_op jit(solution)/shard_map/psum | solution.py:31
  158.0 0.8 reduce.10
  159.0 0.8 reshape.42
  159.9 0.9 slice_reduce_fusion
  160.8 1.7 fusion.5
  162.5 36.9 %scatter_custom_fusion.2 = f32[2048]{0:T(1024)} fusion(s32[6144]{0:T(1024)S(1)} %fusion.5, f32[6144]{0:T(1024)S(1)} %slice_reduce_fusion, f32[]{:T(128)} %constant.30.clone.1), kind=kCustom, calls=%fused_computation.43 | custom fusion | flops 6144 | bytes 8196 | tf_op jit(solution)/shard_map/scatter-add | solution.py:81
  (29 shorter events, 3.3 us)
Async XLA Ops:
  1.9 30.1 %all-to-all-start.1 = ((s32[32,1,3]{2,1,0:T(1,128)}), s32[32,1,3]{2,1,0:T(1,128)S(1)}, u32[]{:S(2)}, u32[]{:S(2)}) async-start(s32[32,1,3]{2,1,0:T(1,128)} %broadcast_in_dim.48), calls=%async_computation.1 | async-start | bytes 32768 | tf_op jit(solution)/shard_map/all_to_all | solution.py:15
  33.4 17.6 %all-to-all-start = ((s32[32,1,1104]{2,1,0:T(1,128)}), s32[32,1,1104]{2,1,0:T(1,128)S(1)}, u32[]{:S(2)}, u32[]{:S(2)}) async-start(s32[32,1,1104]{2,1,0:T(1,128)} %broadcast_in_dim.45), calls=%async_computation | async-start | bytes 294912 | tf_op jit(solution)/shard_map/all_to_all | solution.py:15
  51.5 17.5 %copy-start = (s32[3072,1]{0,1:T(1,128)S(1)}, s32[3072,1]{0,1:T(1,128)}, u32[]{:S(2)}) copy-start(s32[3072,1]{0,1:T(1,128)} %param.7) | copy-start | bytes 36868
  51.6 17.5 %copy-start.1 = (s32[3072]{0:T(1024)S(1)}, s32[3072]{0:T(1024)}, u32[]{:S(2)}) copy-start(s32[3072]{0:T(1024)} %param.9) | copy-start | bytes 36868
  51.6 17.5 %copy-start.2 = (s32[3072]{0:T(1024)S(1)}, s32[3072]{0:T(1024)}, u32[]{:S(2)}) copy-start(s32[3072]{0:T(1024)} %param.8) | copy-start | bytes 36868
  51.6 17.5 %copy-start.4 = (bf16[3072]{0:T(1024)(128)(2,1)S(1)}, bf16[3072]{0:T(1024)(128)(2,1)}, u32[]{:S(2)}) copy-start(bf16[3072]{0:T(1024)(128)(2,1)} %param.10) | copy-start | bytes 18436
  82.0 26.6 %copy-start.5 = (s32[1024]{0:T(1024)S(1)}, s32[1024]{0:T(1024)}, u32[]{:S(2)}) copy-start(s32[1024]{0:T(1024)} %param.13) | copy-start | bytes 12292
  83.9 13.3 %all-to-all-start.2 = ((f32[32,1,384]{2,1,0:T(1,128)}), f32[32,1,384]{2,1,0:T(1,128)S(1)}, u32[]{:S(2)}, u32[]{:S(2)}) async-start(f32[32,1,384]{2,1,0:T(1,128)} %reshape.96), calls=%async_computation.2 | async-start | bytes 98304 | tf_op jit(solution)/shard_map/all_to_all | solution.py:74
  99.5 58.5 %all-to-all-start.3 = ((f32[16,1,768]{2,1,0:T(1,128)}), f32[16,1,768]{2,1,0:T(1,128)S(1)}, u32[]{:S(2)}, u32[]{:S(2)}) async-start(f32[16,1,768]{2,1,0:T(1,128)} %reshape.98), calls=%async_computation.3 | async-start | bytes 98304 | tf_op jit(solution)/shard_map/all_to_all | solution.py:73
  157.4 3.4 %copy-start.3 = (f32[1024]{0:T(1024)}, f32[1024]{0:T(1024)S(1)}, u32[]{:S(2)}) copy-start(f32[1024]{0:T(1024)S(1)} %psum.39) | copy-start | bytes 12292
where the time goes:
time: 200 us; the launch traced here: 199 us
  local copies, waits for them, and re-layouts  50.9 us (25%)
  other arithmetic  48.3 us (24%)
  blocking collectives  46.8 us (23%)
  starting transfers between devices  35.5 us (18%)
  waiting for transfers between devices  15.1 us (8%)
  matrix products  2.01 us (1%)
    psum x5, blocking collectives, over_axes(): x = lax.psum(x, axis)  46.8 us
    scatter-add x1, other arithmetic, per_device(): jax.ops.segment_sum(arrived[:, 0], arrived[:, 1].astype(jnp.int32), num_s...  36.9 us
    all_to_all x2, starting transfers between devices, copy_for_each(): return lax.all_to_all(copies, axis, split_axis=0, concat_axis=0, tiled=True)  21.2 us
    gather x1, local copies, waits for them, and re-layouts, filtered_revenue(): supplier_word = jnp.take(supplier_all, word_index)  17.4 us
    scatter x1, local copies, waits for them, and re-layouts, per_device(): jnp.zeros((devices * capacity,), jnp.float32).at[slot_index]  11.8 us
    scatter x1, local copies, waits for them, and re-layouts, per_device(): slot_offset = jnp.zeros((devices * capacity,), jnp.float32).at[slot_index...  11.8 us
    all_to_all x1, starting transfers between devices, per_device(): lax.all_to_all(lax.all_to_all(payload, COL, split_axis=1, concat_axis=1,...  9.1 us
    all_to_all x1, waiting for transfers between devices, per_device(): lax.all_to_all(payload, COL, split_axis=1, concat_axis=1, tiled=True)  8.08 us
  transfers between devices with their start and end apart: 4, of which 2 were waited for; matrix products, arithmetic and copies ran while one was open for 11% of the time, Pallas kernels for 0%

commit v1 on v0

--- a/solution.py
+++ b/solution.py
@@ -28,7 +28,8 @@
 
 def over_axes(x, axes):
     for axis in axes:
-        x = lax.psum(x, axis)
+        pieces = lax.all_gather(x, axis)
+        x = jnp.sum(pieces, axis=0)
     return x
 
 

time: 200 us -> 218 us (1.090)
  blocking collectives: 46.8 us -> 63.7 us
    all_gather x0 -> x5, blocking collectives: none -> 63.7 us  [over_axes(): pieces = lax.all_gather(x, axis)]
    psum x5 -> x0, blocking collectives: 46.8 us -> none  [over_axes(): x = lax.psum(x, axis)]
where the time goes in v1:
time: 218 us; the launch traced here: 217 us
  blocking collectives  63.7 us (29%)
  local copies, waits for them, and re-layouts  51 us (23%)
  other arithmetic  48.9 us (22%)
  starting transfers between devices  35.5 us (16%)
  waiting for transfers between devices  15.1 us (7%)
    all_gather x5, blocking collectives, over_axes(): pieces = lax.all_gather(x, axis)  63.7 us
    scatter-add x1, other arithmetic, per_device(): jax.ops.segment_sum(arrived[:, 0], arrived[:, 1].astype(jnp.int32), num_s...  36.9 us
    all_to_all x2, starting transfers between devices, copy_for_each(): return lax.all_to_all(copies, axis, split_axis=0, concat_axis=0, tiled=True)  21.2 us
    gather x1, local copies, waits for them, and re-layouts, filtered_revenue(): supplier_word = jnp.take(supplier_all, word_index)  17.4 us
    scatter x1, local copies, waits for them, and re-layouts, per_device(): slot_offset = jnp.zeros((devices * capacity,), jnp.float32).at[slot_index...  11.8 us
    scatter x1, local copies, waits for them, and re-layouts, per_device(): jnp.zeros((devices * capacity,), jnp.float32).at[slot_index]  11.8 us
    all_to_all x1, starting transfers between devices, per_device(): lax.all_to_all(lax.all_to_all(payload, COL, split_axis=1, concat_axis=1,...  9.1 us
    all_to_all x1, waiting for transfers between devices, per_device(): lax.all_to_all(payload, COL, split_axis=1, concat_axis=1, tiled=True)  8.08 us
  transfers between devices with their start and end apart: 4, of which 2 were waited for; matrix products, arithmetic and copies ran while one was open for 11% of the time, Pallas kernels for 0%

profile of v1, /device:TPU:1, one launch (start us, length us, event | category | flops | bytes accessed | tf_op | source)
XLA Modules:
  0.0 217.1 jit_solution(10935652144097117320)
XLA Ops:
  0.6 1.3 broadcast_in_dim.48
  1.9 12.9 %all-to-all-start.1 = ((s32[32,1,3]{2,1,0:T(1,128)}), s32[32,1,3]{2,1,0:T(1,128)S(1)}, u32[]{:S(2)}, u32[]{:S(2)}) async-start(s32[32,1,3]{2,1,0:T(1,128)} %broadcast_in_dim.48), calls=%async_computation.1 | async-start | bytes 32768 | tf_op jit(solution)/shard_map/all_to_all | solution.py:15
  14.8 3.9 %convert_reduce_fusion = s32[3072]{0:T(1024)S(1)} fusion(s32[3072]{0:T(1024)} %bitcast.19), kind=kLoop, calls=%fused_computation.4 | loop fusion | flops 47182848 | bytes 24576 | tf_op jit(solution)/shard_map/reduce_sum | solution.py:62
  18.6 0.7 compare_select_fusion
  19.4 0.8 multiply_add_fusion
  20.2 11.8 %scatter_custom_fusion.1 = f32[6144]{0:T(1024)S(1)} fusion(s32[3072]{0:T(1024)S(1)} %bitcast.24, f32[3072]{0:T(1024)S(1)} %get-tuple-element.7, f32[]{:T(128)} %constant.30.clone.1), kind=kCustom, calls=%fused_computation.33 | custom fusion | bytes 24580 | tf_op jit(solution)/shard_map/scatter | solution.py:70
  32.0 1.4 broadcast_in_dim.45
  33.4 8.3 %all-to-all-start = ((s32[32,1,1104]{2,1,0:T(1,128)}), s32[32,1,1104]{2,1,0:T(1,128)S(1)}, u32[]{:S(2)}, u32[]{:S(2)}) async-start(s32[32,1,1104]{2,1,0:T(1,128)} %broadcast_in_dim.45), calls=%async_computation | async-start | bytes 294912 | tf_op jit(solution)/shard_map/all_to_all | solution.py:15
  41.8 0.7 add_select_fusion.1
  43.0 0.7 reduce.10
  44.1 7.0 %all-to-all-done = s32[32,1,1104]{2,1,0:T(1,128)S(1)} async-done(((s32[32,1,1104]{2,1,0:T(1,128)}), s32[32,1,1104]{2,1,0:T(1,128)S(1)}, u32[]{:S(2)}, u32[]{:S(2)}) %all-to-all-start) | async-done | bytes 141344 | tf_op jit(solution)/shard_map/all_to_all | solution.py:15
  51.6 17.4 %gather_fusion = s32[3072]{0:T(1024)S(1)} fusion(s32[35328]{0:T(1024)S(1)} %reshape.39, s32[3072]{0:T(1024)S(1)} %get-tuple-element.6), kind=kCustom, calls=%fused_computation | custom fusion | bytes 36864 | tf_op jit(solution)/shard_map/jit(_take)/gather | solution.py:39
  69.1 11.8 %scatter_custom_fusion = f32[6144]{0:T(1024)S(1)} fusion(s32[3072]{0:T(1024)S(1)} %bitcast.25, f32[3072]{0:T(1024)S(1)} %get-tuple-element.3, f32[]{:T(128)} %constant.30.clone.1), kind=kCustom, calls=%fused_computation.35 | custom fusion | bytes 24580 | tf_op jit(solution)/shard_map/scatter | solution.py:65
  81.0 1.1 copy.15
  82.0 0.8 reshape.40
  83.0 0.8 reshape.100
  83.9 5.2 %all-to-all-start.2 = ((f32[32,1,384]{2,1,0:T(1,128)}), f32[32,1,384]{2,1,0:T(1,128)S(1)}, u32[]{:S(2)}, u32[]{:S(2)}) async-start(f32[32,1,384]{2,1,0:T(1,128)} %reshape.100), calls=%async_computation.2 | async-start | bytes 98304 | tf_op jit(solution)/shard_map/all_to_all | solution.py:75
  89.1 8.1 %all-to-all-done.2 = f32[32,1,384]{2,1,0:T(1,128)S(1)} async-done(((f32[32,1,384]{2,1,0:T(1,128)}), f32[32,1,384]{2,1,0:T(1,128)S(1)}, u32[]{:S(2)}, u32[]{:S(2)}) %all-to-all-start.2) | async-done | bytes 49184 | tf_op jit(solution)/shard_map/all_to_all | solution.py:75
  97.7 0.8 reduce.11
  98.8 0.8 reshape.102
  99.5 9.1 %all-to-all-start.3 = ((f32[16,1,768]{2,1,0:T(1,128)}), f32[16,1,768]{2,1,0:T(1,128)S(1)}, u32[]{:S(2)}, u32[]{:S(2)}) async-start(f32[16,1,768]{2,1,0:T(1,128)} %reshape.102), calls=%async_computation.3 | async-start | bytes 98304 | tf_op jit(solution)/shard_map/all_to_all | solution.py:74
  108.7 2.0 fusion.1
  110.7 4.9 %all-gather = f32[2048]{0:T(1024)S(1)} all-gather(f32[1024]{0:T(1024)S(1)} %bitcast.27), channel_id=2, replica_groups=mesh['row_0'=2,'row_1'=8,'col_0'=2,'col_1'=8,'col_2'=2] {'row_0'}, dimensions={0}, use_global_device_ids=true | all-gather | bytes 12288 | tf_op jit(solution)/shard_map/all_gather | solution.py:31
  115.6 19.4 %all-gather.1 = f32[8192]{0:T(1024)S(1)} all-gather(f32[1024]{0:T(1024)S(1)} %reduce_sum.77), channel_id=3, replica_groups=mesh['row_0'=2,'row_1'=8,'col_0'=2,'col_1'=8,'col_2'=2] {'row_1'}, dimensions={0}, use_global_device_ids=true | all-gather | bytes 36864 | tf_op jit(solution)/shard_map/all_gather | solution.py:31
  135.0 3.2 %all-gather.2 = f32[2048]{0:T(1024)S(1)} all-gather(f32[1024]{0:T(1024)S(1)} %reduce_sum.78), channel_id=4, replica_groups=mesh['row_0'=2,'row_1'=8,'col_0'=2,'col_1'=8,'col_2'=2] {'col_0'}, dimensions={0}, use_global_device_ids=true | all-gather | bytes 12288 | tf_op jit(solution)/shard_map/all_gather | solution.py:31
  138.3 18.3 %all-gather.3 = f32[8192]{0:T(1024)S(1)} all-gather(f32[1024]{0:T(1024)S(1)} %reduce_sum.79), channel_id=5, replica_groups=mesh['row_0'=2,'row_1'=8,'col_0'=2,'col_1'=8,'col_2'=2] {'col_1'}, dimensions={0}, use_global_device_ids=true | all-gather | bytes 36864 | tf_op jit(solution)/shard_map/all_gather | solution.py:31
  156.6 17.9 %all-gather.4 = f32[2048]{0:T(1024)S(1)} all-gather(f32[1024]{0:T(1024)S(1)} %reduce_sum.80), channel_id=6, replica_groups=mesh['row_0'=2,'row_1'=8,'col_0'=2,'col_1'=8,'col_2'=2] {'col_2'}, dimensions={0}, use_global_device_ids=true | all-gather | bytes 12288 | tf_op jit(solution)/shard_map/all_gather | solution.py:31
  175.7 0.8 reduce.12
  176.7 0.8 reshape.41
  177.5 0.9 slice_reduce_fusion
  178.4 1.7 fusion.5
  180.1 36.9 %scatter_custom_fusion.2 = f32[2048]{0:T(1024)} fusion(s32[6144]{0:T(1024)S(1)} %fusion.5, f32[6144]{0:T(1024)S(1)} %slice_reduce_fusion, f32[]{:T(128)} %constant.30.clone.1), kind=kCustom, calls=%fused_computation.43 | custom fusion | flops 6144 | bytes 8196 | tf_op jit(solution)/shard_map/scatter-add | solution.py:82
  (37 shorter events, 4.0 us)
Async XLA Ops:
  1.9 30.1 %all-to-all-start.1 = ((s32[32,1,3]{2,1,0:T(1,128)}), s32[32,1,3]{2,1,0:T(1,128)S(1)}, u32[]{:S(2)}, u32[]{:S(2)}) async-start(s32[32,1,3]{2,1,0:T(1,128)} %broadcast_in_dim.48), calls=%async_computation.1 | async-start | bytes 32768 | tf_op jit(solution)/shard_map/all_to_all | solution.py:15
  33.4 17.6 %all-to-all-start = ((s32[32,1,1104]{2,1,0:T(1,128)}), s32[32,1,1104]{2,1,0:T(1,128)S(1)}, u32[]{:S(2)}, u32[]{:S(2)}) async-start(s32[32,1,1104]{2,1,0:T(1,128)} %broadcast_in_dim.45), calls=%async_computation | async-start | bytes 294912 | tf_op jit(solution)/shard_map/all_to_all | solution.py:15
  51.5 17.5 %copy-start = (s32[3072,1]{0,1:T(1,128)S(1)}, s32[3072,1]{0,1:T(1,128)}, u32[]{:S(2)}) copy-start(s32[3072,1]{0,1:T(1,128)} %param.7) | copy-start | bytes 36868
  51.6 17.5 %copy-start.1 = (s32[3072]{0:T(1024)S(1)}, s32[3072]{0:T(1024)}, u32[]{:S(2)}) copy-start(s32[3072]{0:T(1024)} %param.9) | copy-start | bytes 36868
  51.6 17.5 %copy-start.2 = (s32[3072]{0:T(1024)S(1)}, s32[3072]{0:T(1024)}, u32[]{:S(2)}) copy-start(s32[3072]{0:T(1024)} %param.8) | copy-start | bytes 36868
  51.6 17.5 %copy-start.3 = (bf16[3072]{0:T(1024)(128)(2,1)S(1)}, bf16[3072]{0:T(1024)(128)(2,1)}, u32[]{:S(2)}) copy-start(bf16[3072]{0:T(1024)(128)(2,1)} %param.10) | copy-start | bytes 18436
  82.0 26.6 %copy-start.4 = (s32[1024]{0:T(1024)S(1)}, s32[1024]{0:T(1024)}, u32[]{:S(2)}) copy-start(s32[1024]{0:T(1024)} %param.13) | copy-start | bytes 12292
  83.9 13.3 %all-to-all-start.2 = ((f32[32,1,384]{2,1,0:T(1,128)}), f32[32,1,384]{2,1,0:T(1,128)S(1)}, u32[]{:S(2)}, u32[]{:S(2)}) async-start(f32[32,1,384]{2,1,0:T(1,128)} %reshape.100), calls=%async_computation.2 | async-start | bytes 98304 | tf_op jit(solution)/shard_map/all_to_all | solution.py:75
  99.5 76.1 %all-to-all-start.3 = ((f32[16,1,768]{2,1,0:T(1,128)}), f32[16,1,768]{2,1,0:T(1,128)S(1)}, u32[]{:S(2)}, u32[]{:S(2)}) async-start(f32[16,1,768]{2,1,0:T(1,128)} %reshape.102), calls=%async_computation.3 | async-start | bytes 98304 | tf_op jit(solution)/shard_map/all_to_all | solution.py:74
